TPU v7x, 32 devices: a 4x2x2 block of a 4x4x8 slice. The times are simulated.
32 devices in a mesh: model: 4 (over y, z), data: 8 (over x, core).
Axes of the slice: x: 4, y: 2, z: 2, core: 2. Of those that a mesh axis runs over, the one named last changes fastest.
The devices are a block of a 4x4x8 slice.
Arguments:
- grad_sq: float32 [32, 12, 256, 256], P(('model', 'data')), parts along dimension 0
- mom_sq: float32 [48, 256, 256], P('model', 'data'), parts along dimension 0
- weight_sq: float32 [48, 256, 256], P('model', 'data'), parts along dimension 0
- grad_kv: float32 [32, 12, 256, 64], P(('model', 'data')), parts along dimension 0
- mom_kv: float32 [48, 256, 64], P('model', 'data'), parts along dimension 0
- weight_kv: float32 [48, 256, 64], P('model', 'data'), parts along dimension 0
- grad_up: float32 [32, 12, 256, 1024], P(('model', 'data')), parts along dimension 0
- mom_up: float32 [48, 256, 1024], P('model', 'data'), parts along dimension 0
- weight_up: float32 [48, 256, 1024], P('model', 'data'), parts along dimension 0
- grad_down: float32 [32, 6, 1024, 256], P(('model', 'data')), parts along dimension 0
- mom_down: float32 [24, 1024, 256], P('model', 'data'), parts along dimension 0
- weight_down: float32 [24, 1024, 256], P('model', 'data'), parts along dimension 0
Outputs:
- output 1: float32 [48, 256, 256], P('model', 'data'), parts along dimension 0
- output 2: float32 [48, 256, 256], P('model', 'data'), parts along dimension 0
- output 3: bfloat16 [48, 256, 256], P('model'), parts along dimension 0
- output 4: float32 [48, 256, 64], P('model', 'data'), parts along dimension 0
- output 5: float32 [48, 256, 64], P('model', 'data'), parts along dimension 0
- output 6: bfloat16 [48, 256, 64], P('model'), parts along dimension 0
- output 7: float32 [48, 256, 1024], P('model', 'data'), parts along dimension 0
- output 8: float32 [48, 256, 1024], P('model', 'data'), parts along dimension 0
- output 9: bfloat16 [48, 256, 1024], P('model'), parts along dimension 0
- output 10: float32 [24, 1024, 256], P('model', 'data'), parts along dimension 0
- output 11: float32 [24, 1024, 256], P('model', 'data'), parts along dimension 0
- output 12: bfloat16 [24, 1024, 256], P('model'), parts along dimension 0
There are 4 independent parts. A program takes and returns all parts, laid end to end along the dimension named above; each array names one.
All inputs are finite; a program needn't handle non-finite values.
Results may differ from a plain program's by a relative error of at most 0.00957222.
Values are sent between devices in bfloat16 or wider.
A program may use at most 768 MiB of HBM per device.

v0:
```python
import math
import jax
import jax.numpy as jnp
from jax import lax
from jax.sharding import PartitionSpec as P, NamedSharding

NS_STEPS = 5
MU = 0.95
LR = 0.1
WD = 0.5
EPS = 1e-7
COEF_A = 3.4445
COEF_B = -4.7750
COEF_C = 2.0315


def orthogonalize(update):
    rows, columns = update.shape[1], update.shape[2]
    update_f32 = update.astype(jnp.float32)
    frob_norm = jnp.sqrt(jnp.sum(update_f32 * update_f32, axis=(1, 2), keepdims=True))
    ortho = (update_f32 / (frob_norm + EPS)).astype(jnp.bfloat16)
    if rows > columns:
        gram_form = "bmk,bmj->bkj"
        apply_form = "bkj,bmj->bmk"
    else:
        gram_form = "bkm,bjm->bkj"
        apply_form = "bkj,bjm->bkm"
    for step_index in range(NS_STEPS):
        gram_mat = jnp.einsum(gram_form, ortho, ortho, preferred_element_type=jnp.float32).astype(jnp.bfloat16)
        square = jnp.einsum("bki,bij->bkj", gram_mat, gram_mat, preferred_element_type=jnp.float32)
        poly_mat = (COEF_B * gram_mat.astype(jnp.float32) + COEF_C * square).astype(jnp.bfloat16)
        ortho = (COEF_A * ortho.astype(jnp.float32) + jnp.einsum(apply_form, poly_mat, ortho, preferred_element_type=jnp.float32)).astype(jnp.bfloat16)
    return ortho


def family_local(grad_part, momentum, weight, group_size):
    count, local_rows, columns = momentum.shape
    rows = local_rows * group_size
    summed = lax.psum_scatter(grad_part[0], "data", scatter_dimension=1, tiled=True) / group_size
    mom_new = MU * momentum + summed
    update = (summed + MU * mom_new).astype(jnp.bfloat16)
    rounds = (count + group_size - 1) // group_size
    filled = jnp.pad(update, ((0, rounds * group_size - count), (0, 0), (0, 0)))
    owned = lax.all_to_all(filled.reshape(rounds, group_size, local_rows, columns), "data", 1, 1, tiled=True)
    ortho = orthogonalize(owned.reshape(rounds, rows, columns))
    returned = lax.all_to_all(ortho.reshape(rounds, group_size, local_rows, columns), "data", 1, 1, tiled=True)
    mine = returned.reshape(rounds * group_size, local_rows, columns)[:count]
    scale = 0.2 * math.sqrt(max(rows, columns))
    weight_new = weight - LR * (scale * mine.astype(jnp.float32) + WD * weight)
    gathered = lax.all_gather(weight_new.astype(jnp.bfloat16), "data", axis=1, tiled=True)
    return mom_new, weight_new, gathered


def solution(mesh):
    group_size = mesh.shape["data"]
    grad_spec = P(("model", "data"))
    slab_spec = P("model", "data")
    full_spec = P("model")

    def local_step(*arrays):
        results = []
        for family_index in range(4):
            results.extend(family_local(arrays[3 * family_index], arrays[3 * family_index + 1], arrays[3 * family_index + 2], group_size))
        return tuple(results)

    in_specs = (grad_spec, slab_spec, slab_spec) * 4
    out_specs = (slab_spec, slab_spec, full_spec) * 4
    return jax.shard_map(local_step, mesh=mesh, in_specs=in_specs, out_specs=out_specs, check_vma=False)
```

profile of v0, /device:TPU:81, one launch (start us, length us, event | category | flops | bytes accessed | tf_op | source)
XLA Modules:
  0.0 324.0 jit_solution(8345845113659622491)
XLA Ops:
  7.3 0.7 reduce-scatter.5.cloned.1.call-update
  8.1 0.7 reduce-scatter.11.cloned.1.call-update
  8.9 0.7 reduce-scatter.9.cloned.1.call-update
  9.6 34.6 %reduce-scatter.5.cloned.1.call-done = f32[12,32,256]{2,1,0:T(8,128)} async-done(((f32[12,256,256]{2,1,0:T(8,128)}), f32[12,32,256]{2,1,0:T(8,128)}) %reduce-scatter.5.cloned.1.call-update) | async-done | bytes 393232 | tf_op jit(solution)/shard_map/reduce_scatter | solution.py:39
  44.2 1.8 add_convert_fusion.7
  46.0 0.7 copy.47
  46.7 7.2 %all-to-all-start = ((bf16[2,8,32,256]{3,2,0,1:T(8,128)(2,1)}), bf16[2,8,32,256]{3,2,0,1:T(8,128)(2,1)S(1)}, u32[]{:S(2)}, u32[]{:S(2)}) async-start(bf16[2,8,32,256]{3,2,0,1:T(8,128)(2,1)} %copy.47), calls=%async_computation.1 | async-start | bytes 524288 | tf_op jit(solution)/shard_map/all_to_all | solution.py:44
  53.9 1.6 copy.51
  55.6 6.4 %all-to-all-done = bf16[2,8,32,256]{3,2,0,1:T(8,128)(2,1)S(1)} async-done(((bf16[2,8,32,256]{3,2,0,1:T(8,128)(2,1)}), bf16[2,8,32,256]{3,2,0,1:T(8,128)(2,1)S(1)}, u32[]{:S(2)}, u32[]{:S(2)}) %all-to-all-start) | async-done | bytes 262176 | tf_op jit(solution)/shard_map/all_to_all | solution.py:44
  62.7 0.4 fusion.26
  63.3 0.4 fusion.27
  63.9 0.4 fusion.28
  64.6 0.4 fusion.29
  65.2 0.4 fusion.30
  65.6 0.7 copy.49
  66.3 4.3 %all-to-all-start.1 = ((bf16[2,8,32,256]{3,2,0,1:T(8,128)(2,1)}), bf16[2,8,32,256]{3,2,0,1:T(8,128)(2,1)S(1)}, u32[]{:S(2)}, u32[]{:S(2)}) async-start(bf16[2,8,32,256]{3,2,0,1:T(8,128)(2,1)} %copy.49), calls=%async_computation.2 | async-start | bytes 524288 | tf_op jit(solution)/shard_map/all_to_all | solution.py:46
  70.6 22.4 %reduce-scatter.11.cloned.1.call-done = f32[6,128,256]{2,1,0:T(8,128)} async-done(((f32[6,1024,256]{2,1,0:T(8,128)}), f32[6,128,256]{2,1,0:T(8,128)}) %reduce-scatter.11.cloned.1.call-update) | async-done | bytes 786448 | tf_op jit(solution)/shard_map/reduce_scatter | solution.py:39
  93.0 2.2 add_convert_fusion.6
  95.2 0.8 pad_bitcast_fusion
  96.0 4.7 %all-to-all-start.6 = ((bf16[1,8,128,256]{3,2,0,1:T(8,128)(2,1)}), bf16[1,8,128,256]{3,2,0,1:T(8,128)(2,1)S(1)}, u32[]{:S(2)}, u32[]{:S(2)}) async-start(bf16[1,8,128,256]{3,2,0,1:T(8,128)(2,1)} %pad_bitcast_fusion), calls=%async_computation.10 | async-start | bytes 1048576 | tf_op jit(solution)/shard_map/all_to_all | solution.py:44
  100.7 0.9 fusion.187
  101.7 11.3 %all-to-all-done.6 = bf16[1,8,128,256]{3,2,0,1:T(8,128)(2,1)S(1)} async-done(((bf16[1,8,128,256]{3,2,0,1:T(8,128)(2,1)}), bf16[1,8,128,256]{3,2,0,1:T(8,128)(2,1)S(1)}, u32[]{:S(2)}, u32[]{:S(2)}) %all-to-all-start.6) | async-done | bytes 524320 | tf_op jit(solution)/shard_map/all_to_all | solution.py:44
  113.0 0.9 fusion.57
  114.7 0.3 fusion.41
  115.1 0.5 fusion.1
  115.6 0.3 convolution_convert_fusion.13
  115.9 0.5 fusion.2
  116.4 0.3 convolution_convert_fusion.12
  116.8 0.5 fusion.3
  117.3 0.3 convolution_convert_fusion.11
  117.6 0.5 fusion.4
  118.2 0.3 convolution_convert_fusion.10
  118.5 1.3 fusion.5
  119.8 4.3 %all-to-all-start.7 = ((bf16[1,8,128,256]{3,2,0,1:T(8,128)(2,1)}), bf16[1,8,128,256]{3,2,0,1:T(8,128)(2,1)S(1)}, u32[]{:S(2)}, u32[]{:S(2)}) async-start(bf16[1,8,128,256]{3,2,0,1:T(8,128)(2,1)} %bitcast.22), calls=%async_computation.11 | async-start | bytes 1048576 | tf_op jit(solution)/shard_map/all_to_all | solution.py:46
  124.1 51.1 %reduce-scatter.9.cloned.1.call-done = f32[12,32,1024]{2,1,0:T(8,128)} async-done(((f32[12,256,1024]{2,1,0:T(8,128)}), f32[12,32,1024]{2,1,0:T(8,128)}) %reduce-scatter.9.cloned.1.call-update) | async-done | bytes 1572880 | tf_op jit(solution)/shard_map/reduce_scatter | solution.py:39
  175.3 2.9 add_convert_fusion.5
  178.4 1.1 copy.58
  179.4 5.0 %all-to-all-start.4 = ((bf16[2,8,32,1024]{3,2,0,1:T(8,128)(2,1)}), bf16[2,8,32,1024]{3,2,0,1:T(8,128)(2,1)S(1)}, u32[]{:S(2)}, u32[]{:S(2)}) async-start(bf16[2,8,32,1024]{3,2,0,1:T(8,128)(2,1)} %copy.58), calls=%async_computation.7 | async-start | bytes 2097152 | tf_op jit(solution)/shard_map/all_to_all | solution.py:44
  184.5 1.2 fusion.183
  186.0 17.6 %all-to-all-done.4 = bf16[2,8,32,1024]{3,2,0,1:T(8,128)(2,1)S(1)} async-done(((bf16[2,8,32,1024]{3,2,0,1:T(8,128)(2,1)}), bf16[2,8,32,1024]{3,2,0,1:T(8,128)(2,1)S(1)}, u32[]{:S(2)}, u32[]{:S(2)}) %all-to-all-start.4) | async-done | bytes 1048608 | tf_op jit(solution)/shard_map/all_to_all | solution.py:44
  203.8 0.4 multiply_reduce_fusion
  204.2 0.3 fusion
  204.5 0.5 convolution_convert_fusion.4
  205.0 0.6 add_convert_fusion.4
  205.6 0.5 convolution_convert_fusion.3
  206.1 0.6 add_convert_fusion.3
  206.7 0.5 convolution_convert_fusion.2
  207.2 0.6 add_convert_fusion.2
  207.8 0.5 convolution_convert_fusion.1
  208.2 0.6 add_convert_fusion.1
  208.8 0.5 convolution_convert_fusion
  209.3 0.6 add_convert_fusion
  210.0 23.6 %all_to_all.40 = bf16[2,8,32,1024]{3,2,0,1:T(8,128)(2,1)S(1)} all-to-all(bf16[2,8,32,1024]{3,2,0,1:T(8,128)(2,1)S(1)} %copy.60), channel_id=1, replica_groups=mesh['model'=4,'data'=8] {'data'}, dimensions={1} | all-to-all | bytes 2097152 | tf_op jit(solution)/shard_map/all_to_all | solution.py:46
  233.8 1.8 fusion.185
  235.6 1.7 add_convert_fusion.8
  237.5 8.9 %all_to_all.41 = bf16[8,2,2048]{2,1,0:T(2,128)(2,1)S(1)} all-to-all(bf16[8,2,2048]{2,1,0:T(2,128)(2,1)S(1)} %reshape.260), channel_id=1, replica_groups=mesh['model'=4,'data'=8] {'data'}, dimensions={0} | all-to-all | bytes 131072 | tf_op jit(solution)/shard_map/all_to_all | solution.py:44
  249.3 8.7 %all_to_all.42 = bf16[8,2,2048]{2,1,0:T(2,128)(2,1)S(1)} all-to-all(bf16[8,2,2048]{2,1,0:T(2,128)(2,1)S(1)} %reshape.262), channel_id=1, replica_groups=mesh['model'=4,'data'=8] {'data'}, dimensions={0} | all-to-all | bytes 131072 | tf_op jit(solution)/shard_map/all_to_all | solution.py:46
  258.3 0.7 fusion.186
  259.0 14.2 %all_gather.13 = bf16[12,256,64]{2,1,0:T(8,128)(2,1)S(1)} all-gather(bf16[12,32,64]{2,1,0:T(8,128)(2,1)S(1)} %get-tuple-element.44), channel_id=1, replica_groups=mesh['model'=4,'data'=8] {'data'}, dimensions={1}, use_global_device_ids=true | all-gather | bytes 442368 | tf_op jit(solution)/shard_map/all_gather | solution.py:50
  273.2 1.0 copy.65
  274.2 32.2 %all-gather.6.cloned.1.call-done = bf16[12,256,1024]{2,1,0:T(8,128)(2,1)} async-done(((bf16[12,32,1024]{2,1,0:T(8,128)(2,1)}), bf16[12,256,1024]{2,1,0:T(8,128)(2,1)}) %all-gather.6.cloned.1.call-update) | async-done | bytes 6291472 | tf_op jit(solution)/shard_map/all_gather | solution.py:50
  306.4 2.7 copy.74
  309.1 6.4 %copy.75 = bf16[12,256,1024]{2,1,0:T(8,128)(2,1)} copy(bf16[12,256,1024]{2,1,0:T(8,128)(2,1)} %all-gather.6.cloned.1.call-done) | data formatting | bytes 12582912
  315.4 1.7 copy.76
  (77 shorter events, 6.2 us)
Async XLA Ops:
  7.2 37.0 %reduce-scatter.5.cloned.1.call-start = ((), (), s32[]{:S(2)}) async-start(), calls=%async_computation.12 | async-start | bytes 3538944 | tf_op jit(solution)/shard_map/reduce_scatter | solution.py:39
  8.0 85.0 %reduce-scatter.11.cloned.1.call-start = ((), (), s32[]{:S(2)}) async-start(), calls=%async_computation.17 | async-start | bytes 7077888 | tf_op jit(solution)/shard_map/reduce_scatter | solution.py:39
  8.8 166.5 %reduce-scatter.9.cloned.1.call-start = ((), (), s32[]{:S(2)}) async-start(), calls=%async_computation.15 | async-start | bytes 14155776 | tf_op jit(solution)/shard_map/reduce_scatter | solution.py:39
  8.9 35.3 %copy-start.6 = (f32[12,32,256]{2,1,0:T(8,128)S(1)}, f32[12,32,256]{2,1,0:T(8,128)}, u32[]{:S(2)}) copy-start(f32[12,32,256]{2,1,0:T(8,128)} %param.13) | copy-start | bytes 1179652
  9.6 44.4 %copy-start.3 = (f32[1,12,256,64]{2,3,1,0:T(8,128)S(1)}, f32[1,12,256,64]{2,3,1,0:T(8,128)}, u32[]{:S(2)}) copy-start(f32[1,12,256,64]{2,3,1,0:T(8,128)} %param.15) | copy-start | bytes 2359300
  46.7 15.3 %all-to-all-start = ((bf16[2,8,32,256]{3,2,0,1:T(8,128)(2,1)}), bf16[2,8,32,256]{3,2,0,1:T(8,128)(2,1)S(1)}, u32[]{:S(2)}, u32[]{:S(2)}) async-start(bf16[2,8,32,256]{3,2,0,1:T(8,128)(2,1)} %copy.47), calls=%async_computation.1 | async-start | bytes 524288 | tf_op jit(solution)/shard_map/all_to_all | solution.py:44
  53.9 181.7 %reduce-scatter.7.cloned.1.call-start = ((), (), s32[]{:S(2)}) async-start(), calls=%async_computation.14 | async-start | bytes 1769472 | tf_op jit(solution)/shard_map/reduce_scatter | solution.py:39
  64.6 28.4 %copy-start.4 = (f32[6,128,256]{2,1,0:T(8,128)S(1)}, f32[6,128,256]{2,1,0:T(8,128)}, u32[]{:S(2)}) copy-start(f32[6,128,256]{2,1,0:T(8,128)} %param.22) | copy-start | bytes 2359300
  66.3 29.7 %all-to-all-start.1 = ((bf16[2,8,32,256]{3,2,0,1:T(8,128)(2,1)}), bf16[2,8,32,256]{3,2,0,1:T(8,128)(2,1)S(1)}, u32[]{:S(2)}, u32[]{:S(2)}) async-start(bf16[2,8,32,256]{3,2,0,1:T(8,128)(2,1)} %copy.49), calls=%async_computation.2 | async-start | bytes 524288 | tf_op jit(solution)/shard_map/all_to_all | solution.py:46
  70.6 30.1 %copy-start.7 = (f32[12,32,256]{2,1,0:T(8,128)S(1)}, f32[12,32,256]{2,1,0:T(8,128)}, u32[]{:S(2)}) copy-start(f32[12,32,256]{2,1,0:T(8,128)} %param.14) | copy-start | bytes 1179652
  96.0 17.0 %all-to-all-start.6 = ((bf16[1,8,128,256]{3,2,0,1:T(8,128)(2,1)}), bf16[1,8,128,256]{3,2,0,1:T(8,128)(2,1)S(1)}, u32[]{:S(2)}, u32[]{:S(2)}) async-start(bf16[1,8,128,256]{3,2,0,1:T(8,128)(2,1)} %pad_bitcast_fusion), calls=%async_computation.10 | async-start | bytes 1048576 | tf_op jit(solution)/shard_map/all_to_all | solution.py:44
  100.7 173.5 %all-gather.4.cloned.1.call-start = ((), (), s32[]{:S(2)}) async-start(), calls=%async_computation.13 | async-start | bytes 1769472 | tf_op jit(solution)/shard_map/all_gather | solution.py:50
  118.1 57.1 %copy-start.1 = (f32[12,32,1024]{2,1,0:T(8,128)S(1)}, f32[12,32,1024]{2,1,0:T(8,128)}, u32[]{:S(2)}) copy-start(f32[12,32,1024]{2,1,0:T(8,128)} %param.19) | copy-start | bytes 4718596
  119.8 59.6 %all-to-all-start.7 = ((bf16[1,8,128,256]{3,2,0,1:T(8,128)(2,1)}), bf16[1,8,128,256]{3,2,0,1:T(8,128)(2,1)S(1)}, u32[]{:S(2)}, u32[]{:S(2)}) async-start(bf16[1,8,128,256]{3,2,0,1:T(8,128)(2,1)} %bitcast.22), calls=%async_computation.11 | async-start | bytes 1048576 | tf_op jit(solution)/shard_map/all_to_all | solution.py:46
  178.3 6.1 %copy-start.5 = (f32[6,128,256]{2,1,0:T(8,128)S(1)}, f32[6,128,256]{2,1,0:T(8,128)}, u32[]{:S(2)}) copy-start(f32[6,128,256]{2,1,0:T(8,128)} %param.23) | copy-start | bytes 2359300
  179.4 24.1 %all-to-all-start.4 = ((bf16[2,8,32,1024]{3,2,0,1:T(8,128)(2,1)}), bf16[2,8,32,1024]{3,2,0,1:T(8,128)(2,1)S(1)}, u32[]{:S(2)}, u32[]{:S(2)}) async-start(bf16[2,8,32,1024]{3,2,0,1:T(8,128)(2,1)} %copy.58), calls=%async_computation.7 | async-start | bytes 2097152 | tf_op jit(solution)/shard_map/all_to_all | solution.py:44
  184.5 89.8 %all-gather.8.cloned.1.call-start = ((), (), s32[]{:S(2)}) async-start(), calls=%async_computation.18 | async-start | bytes 3538944 | tf_op jit(solution)/shard_map/all_gather | solution.py:50
  185.7 120.7 %all-gather.6.cloned.1.call-start = ((), (), s32[]{:S(2)}) async-start(), calls=%async_computation.16 | async-start | bytes 7077888 | tf_op jit(solution)/shard_map/all_gather | solution.py:50
  210.0 23.7 %copy-start.2 = (f32[12,32,1024]{2,1,0:T(8,128)S(1)}, f32[12,32,1024]{2,1,0:T(8,128)}, u32[]{:S(2)}) copy-start(f32[12,32,1024]{2,1,0:T(8,128)} %param.20) | copy-start | bytes 4718596
  233.8 1.9 copy-start.8
  246.5 11.7 %copy-start.9 = (f32[12,32,64]{2,1,0:T(8,128)S(1)}, f32[12,32,64]{2,1,0:T(8,128)}, u32[]{:S(2)}) copy-start(f32[12,32,64]{2,1,0:T(8,128)} %param.17) | copy-start | bytes 294916
  309.1 6.4 %copy-start = (bf16[6,1024,256]{2,1,0:T(8,128)(2,1)S(1)}, bf16[6,1024,256]{2,1,0:T(8,128)(2,1)}, u32[]{:S(2)}) copy-start(bf16[6,1024,256]{2,1,0:T(8,128)(2,1)} %all-gather.8.cloned.1.call-done) | copy-start | bytes 9437188
Sparse Core Ops, SparseCore 0:
  10.3 33.7 reduce-scatter.4
  46.5 46.4 reduce-scatter.10
  95.3 79.9 reduce-scatter.8
  178.0 31.8 reduce-scatter.6
  211.4 26.1 all-gather.3
  239.6 26.8 all-gather.7
  268.7 37.7 all-gather.5
where the time goes:
time: 325 us; the launch traced here: 324 us
  waiting for transfers between devices  178 us (55%)
  blocking collectives  55.5 us (17%)
  starting transfers between devices  26 us (8%)
  local copies, waits for them, and re-layouts  18.2 us (6%)
  matrix products  15.5 us (5%)
  other arithmetic  15.4 us (5%)
  between operations  15.3 us (5%)
    reduce_scatter x4, waiting for transfers between devices, family_local(): lax.psum_scatter(grad_part[0], 'data', scatter_dimension=1, tiled=True)  108 us
    all_to_all x3, waiting for transfers between devices, family_local(): lax.all_to_all(filled.reshape(rounds, group_size, local_rows, columns), '...  35.4 us
    all_to_all x2, blocking collectives, family_local(): lax.all_to_all(ortho.reshape(rounds, group_size, local_rows, columns), 'd...  32.4 us
    all_gather x3, waiting for transfers between devices, family_local(): lax.all_gather(weight_new.astype(jnp.bfloat16), 'data', axis=1, tiled=True)  32.2 us
    all_to_all x3, starting transfers between devices, family_local(): lax.all_to_all(filled.reshape(rounds, group_size, local_rows, columns), '...  16.9 us
    all_gather x1, blocking collectives, family_local(): lax.all_gather(weight_new.astype(jnp.bfloat16), 'data', axis=1, tiled=True)  14.2 us
    unnamed x29, local copies, waits for them, and re-layouts  14 us
    dot_general x20, matrix products, orthogonalize(): jnp.einsum(apply_form, poly_mat, ortho, preferred_element_type=jnp.float32)  9.48 us
  transfers between devices with their start and end apart: 12, of which 7 were waited for; matrix products, arithmetic and copies ran while one was open for 12% of the time, Pallas kernels for 0%

commit v1 on v0

v1 whole, which is shorter than its diff:
```python
import math

import jax
import jax.numpy as jnp
from jax import lax
from jax.experimental import pallas as pl
from jax.experimental.pallas import tpu as pltpu
from jax.sharding import PartitionSpec as P

NS_STEPS = 5
MU = 0.95
LR = 0.1
WD = 0.5
EPS = 1e-7
COEF_A = 3.4445
COEF_B = -4.7750
COEF_C = 2.0315
F32 = jnp.float32
BF16 = jnp.bfloat16
MESH = pl.DeviceIdType.MESH
NT = (((1,), (1,)), ((), ()))
PACK = 4

PIECES = (
    ("u", 0, 1, 2), ("u", 2, 3, 4), ("u", 4, 5, 6), ("u", 6, 7, 8), ("u", 8, 9, 10), ("u", 10, 11, 12),
    ("w", 0, 1, 2), ("w", 2, 3, 4), ("w", 4, 5, 6), ("s", 0, 4, 8), ("s", 8, 12, 15),
)
GROUPS = (
    ("u", 0, 2, 4), ("u", 4, 6, 8), ("u", 8, 10, 12), ("w", 0, 2, 4), ("w", 4, 5, 6), ("s", 0, 4, 8), ("s", 8, 12, 15),
)
OWNER = {
    "u": tuple((j, 0) for j in range(8)) + tuple((j, 1) for j in range(4)),
    "w": tuple((4 + j, 0) for j in range(4)) + ((0, 1), (2, 1)),
    "s": tuple((dev, slot) for dev in (1, 3, 4, 5, 6, 7) for slot in (0, 1)) + ((4, 2), (5, 2), (6, 2)),
}
FIRST = {"u": 0, "w": 12, "s": 18}
PEER_SEMS = 6


def muon_kernel(n, nx, sq_count, *refs):
    (g_sq, g_kv, g_up, g_dn, m_sq, m_kv, m_up, m_dn, w_sq, w_kv, w_up, w_dn,
     om_sq, ow_sq, ob_sq, om_kv, ow_kv, ob_kv, om_up, ow_up, ob_up, om_dn, ow_dn, ob_dn,
     p_s, p_u, p_w, q_s, q_u, q_w, pk, qk,
     t_s, t_u, t_w, l_s, l_u, l_w, r_s, r_u, r_w,
     mv_s, mv_k, mv_u, mv_w, wv_s, wv_k, wv_u, wv_w,
     us_s, us_u, us_w, uo_s, uo_u, uo_w, xr_s, xr_u, xr_w, f_s, f_u, f_w, fk, xt, xs,
     sem_load, sem_mw, sem_peer_s, sem_peer_r, sem_kv, sem_st_s, sem_st_r, sem_us, sem_ur,
     sem_xs, sem_xr, sem_gs, sem_gr, sem_out, sem_outb) = refs
    part = {"s": p_s, "u": p_u, "w": p_w}
    other = {"s": q_s, "u": q_u, "w": q_w}
    opp = {"s": t_s, "u": t_u, "w": t_w}
    from_l = {"s": l_s, "u": l_u, "w": l_w}
    from_r = {"s": r_s, "u": r_u, "w": r_w}
    grad = {"s": g_sq, "u": g_up, "w": g_dn}
    mom = {"s": mv_s, "u": mv_u, "w": mv_w}
    wei = {"s": wv_s, "u": wv_u, "w": wv_w}
    u_send = {"s": us_s, "u": us_u, "w": us_w}
    u_own = {"s": uo_s, "u": uo_u, "w": uo_w}
    x_recv = {"s": xr_s, "u": xr_u, "w": xr_w}
    full = {"s": f_s, "u": f_u, "w": f_w}
    out_m = {"s": om_sq, "u": om_up, "w": om_dn}
    out_w = {"s": ow_sq, "u": ow_up, "w": ow_dn}
    out_b = {"s": ob_sq, "u": ob_up, "w": ob_dn}
    scale = {
        "s": 0.2 * math.sqrt(n * m_sq.shape[1]),
        "u": 0.2 * math.sqrt(m_up.shape[2]),
        "w": 0.2 * math.sqrt(n * m_dn.shape[1]),
    }

    d = lax.axis_index("data")
    x = d // 2
    c = lax.rem(d, 2)
    xr = lax.rem(x + 1, nx)
    xl = lax.rem(x + nx - 1, nx)
    xo = lax.rem(x + 2, nx)
    right, left, peer = 2 * xr + c, 2 * xl + c, 2 * x + 1 - c

    def remote(src, dst, ssem, rsem, dev):
        return pltpu.make_async_remote_copy(
            src_ref=src, dst_ref=dst, send_sem=ssem, recv_sem=rsem, device_id={"data": dev}, device_id_type=MESH)

    def arrived(dst, rsem):
        remote(dst, dst, sem_gs.at[0, 0], rsem, peer).wait_recv()

    sent = []

    def send(src, dst, ssem, rsem, dev, cond=None):
        copy = remote(src, dst, ssem, rsem, dev)
        if cond is None:
            copy.start()
        else:
            pl.when(cond)(copy.start)
        sent.append((copy, cond))

    local = []

    def store(src, dst, sem):
        copy = pltpu.make_async_copy(src, dst, sem)
        copy.start()
        local.append(copy)

    loads = []
    for p, (f, j0, jm, j1) in enumerate(PIECES):
        e1 = min(j1, sq_count) if f == "s" else j1
        copy = pltpu.make_async_copy(grad[f].at[pl.ds(j0, e1 - j0), :, c], part[f].at[pl.ds(j0, e1 - j0)], sem_load.at[p])
        copy.start()
        loads.append(copy)
    load_kv = pltpu.make_async_copy(g_kv, pk, sem_kv.at[0])
    load_kv.start()
    mw_loads = {}
    for i, (key, src, dst) in enumerate((
            ("mu", m_up, mv_u), ("wu", w_up, wv_u), ("mw", m_dn, mv_w), ("ww", w_dn, wv_w),
            ("ms", m_sq, mv_s.at[pl.ds(0, sq_count)]), ("ws", w_sq, wv_s), ("mk", m_kv, mv_k), ("wk", w_kv, wv_k))):
        copy = pltpu.make_async_copy(src, dst, sem_mw.at[i])
        copy.start()
        mw_loads[key] = copy

    barrier = pltpu.get_barrier_semaphore()
    for k in range(1, n):
        pl.semaphore_signal(barrier, inc=1, device_id={"data": lax.rem(d + k, n)}, device_id_type=MESH)
    pl.semaphore_wait(barrier, n - 1)

    for p, (f, j0, jm, j1) in enumerate(PIECES):
        e1 = min(j1, sq_count) if f == "s" else j1
        send(grad[f].at[pl.ds(j0, e1 - j0), :, 1 - c], other[f].at[pl.ds(j0, e1 - j0)],
             sem_peer_s.at[p], sem_peer_r.at[p], peer)
    send(g_kv, qk, sem_kv.at[1], sem_kv.at[2], peer)

    def stage_a(p):
        f, j0, jm, j1 = PIECES[p]
        e1 = min(j1, sq_count) if f == "s" else j1
        loads[p].wait()
        arrived(other[f].at[pl.ds(j0, e1 - j0)], sem_peer_r.at[p])
        pr, ot = part[f], other[f]
        if f == "s":
            def add(j, carry):
                pr[j] = pr[j] + ot[j]
                return carry
            lax.fori_loop(j0, e1, add, 0)
            if j1 > sq_count:
                load_kv.wait()
                arrived(qk, sem_kv.at[2])
                rows, lanes = p_s.shape[2], p_s.shape[3]
                for i in range(j1 - sq_count):
                    t = jnp.transpose(pk[i] + qk[i]).reshape(nx, 2, rows, lanes)
                    pr[sq_count + i] = jnp.where(c == 0, t[:, 0], t[:, 1])
        else:
            def add(t, carry):
                j, xi = j0 + t // nx, lax.rem(t, nx)
                pr[j, xi] = pr[j, xi] + ot[j, xi]
                return carry
            lax.fori_loop(0, (j1 - j0) * nx, add, 0)
        a, b = pl.ds(j0, jm - j0), pl.ds(jm, j1 - jm)
        send(pr.at[a, xo], opp[f].at[a], sem_st_s.at[p, 0], sem_st_r.at[p, 0], right)
        send(pr.at[b, xo], opp[f].at[b], sem_st_s.at[p, 1], sem_st_r.at[p, 1], left)
        send(pr.at[b, xr], from_l[f].at[b], sem_st_s.at[p, 2], sem_st_r.at[p, 2], right)
        send(pr.at[a, xl], from_r[f].at[a], sem_st_s.at[p, 3], sem_st_r.at[p, 3], left)

    def stage_b(p):
        f, j0, jm, j1 = PIECES[p]
        op, pr = opp[f], part[f]
        for half, (lo, hi, to, dev, dst) in enumerate(((j0, jm, xr, right, from_l), (jm, j1, xl, left, from_r))):
            r = pl.ds(lo, hi - lo)
            arrived(op.at[r], sem_st_r.at[p, half])

            def add(j, carry):
                op[j] = op[j] + pr[j, to]
                return carry
            lax.fori_loop(lo, hi, add, 0)
            send(op.at[r], dst[f].at[r], sem_st_s.at[p, 4 + half], sem_st_r.at[p, 4 + half], dev)

    def stage_c(p):
        f, j0, jm, j1 = PIECES[p]
        a, b = pl.ds(j0, jm - j0), pl.ds(jm, j1 - jm)
        for key in ("m" + f, "mk" if j1 > sq_count else None):
            if key in mw_loads:
                mw_loads.pop(key).wait()
        arrived(from_l[f].at[b], sem_st_r.at[p, 2])
        arrived(from_r[f].at[a], sem_st_r.at[p, 3])
        arrived(from_l[f].at[a], sem_st_r.at[p, 4])
        arrived(from_r[f].at[b], sem_st_r.at[p, 5])
        if j1 > sq_count:
            wide = m_kv.shape[2]
            for i in range(j1 - sq_count):
                mv_s[sq_count + i] = jnp.concatenate([mv_k[PACK * i + k] for k in range(PACK)], axis=-1)

        def update(j, carry):
            g = ((part[f][j, x] + from_l[f][j]) + from_r[f][j]) * (1.0 / n)
            m = MU * mom[f][j] + g
            mom[f][j] = m
            u_send[f][j] = (g + MU * m).astype(BF16)
            return carry
        lax.fori_loop(j0, j1, update, 0)
        for j in range(j0, j1):
            dev, slot = OWNER[f][j]
            send(u_send[f].at[j], u_own[f].at[slot, d], sem_us.at[FIRST[f] + j], sem_ur.at[FIRST[f] // 6, slot], dev, d != dev)
        e1 = min(j1, sq_count) if f == "s" else j1
        r = pl.ds(j0, e1 - j0)
        store(mom[f].at[r], out_m[f].at[r], sem_out.at[p, 0])
        if j1 > sq_count:
            for i in range(j1 - sq_count):
                for k in range(PACK):
                    mv_k[PACK * i + k] = mv_s[sq_count + i, :, wide * k:wide * (k + 1)]
            store(mv_k, om_kv, sem_out.at[p, 1])

    def take(f, slot, j):
        rows = u_own[f].at[slot, pl.ds(0, n - 1)]
        arrived(rows, sem_ur.at[FIRST[f] // 6, slot])
        u_own[f][slot, d] = u_send[f][j]

    def give(f, slot, j, base):
        for k in range(1, n):
            to = lax.rem(d + k, n)
            copy = remote(u_own[f].at[slot, to], x_recv[f].at[j], sem_xs.at[base, k - 1], sem_xr.at[FIRST[f] + j], to)
            copy.start()
        x_recv[f][j] = u_own[f][slot, d]

    def given(f, slot, j, base):
        for k in range(1, n):
            to = lax.rem(d + k, n)
            remote(u_own[f].at[slot, to], x_recv[f].at[j], sem_xs.at[base, k - 1], sem_xr.at[FIRST[f] + j], to).wait_send()

    xt_rows = xt.shape[1]

    def frob(ref):
        def square(i, acc):
            v = ref[i].astype(F32)
            return acc + v * v
        total = lax.fori_loop(0, n, square, jnp.zeros(ref.shape[1:], F32))
        return jnp.sqrt(jnp.sum(total, axis=(0, 1), keepdims=True)) + EPS

    def start_up(slot):
        ref = u_own["u"].at[slot]
        norm = frob(ref)
        for i in range(n):
            xt[i] = (ref[i].astype(F32) / norm).astype(BF16)

    def end_up(slot):
        for i in range(n):
            u_own["u"][slot, i] = xt[i]

    def start_dn(slot):
        ref = u_own["w"].at[slot]
        norm = frob(ref)
        width = ref.shape[1]
        for i in range(n):
            t = jnp.transpose(ref[i].astype(F32) / norm).astype(BF16)
            xt[:, :, width * i:width * (i + 1)] = t.reshape(n, xt_rows, width)

    def end_dn(slot):
        width = u_own["w"].shape[2]
        for i in range(n):
            t = xt[:, :, width * i:width * (i + 1)].reshape(n * xt_rows, width)
            u_own["w"][slot, i] = jnp.transpose(t.astype(F32)).astype(BF16)

    def ns_large():
        k, l = n * xt_rows, xt.shape[2]

        def step(_, carry):
            v = xt[...].reshape(k, l)
            gram = lax.dot_general(v, v, NT, preferred_element_type=F32).astype(BF16)
            square = jnp.dot(gram, gram, preferred_element_type=F32)
            poly = (COEF_B * gram.astype(F32) + COEF_C * square).astype(BF16)
            for i in range(0, l, k):
                v = xt[:, :, i:i + k].reshape(k, k)
                y = COEF_A * v.astype(F32) + jnp.dot(poly, v, preferred_element_type=F32)
                xt[:, :, i:i + k] = y.astype(BF16).reshape(n, xt_rows, k)
            return carry
        lax.fori_loop(0, NS_STEPS, step, 0)

    def ns_small(slots, mask):
        def step(_, carry):
            for s in slots:
                v = xs[s]
                gram = lax.dot_general(v, v, NT, preferred_element_type=F32)
                if mask is not None:
                    gram = jnp.where(mask, gram, 0.0)
                gram = gram.astype(BF16)
                square = jnp.dot(gram, gram, preferred_element_type=F32)
                poly = (COEF_B * gram.astype(F32) + COEF_C * square).astype(BF16)
                xs[s] = (COEF_A * v.astype(F32) + jnp.dot(poly, v, preferred_element_type=F32)).astype(BF16)
            return carry
        lax.fori_loop(0, NS_STEPS, step, 0)

    def round_a():
        take("u", 0, d)
        start_up(0)
        ns_large()
        end_up(0)
        give("u", 0, d, 0)

    half = n // 2

    def round_b():
        @pl.when(d < half)
        def _():
            take("u", 1, n + d)
            start_up(1)

        @pl.when(d >= half)
        def _():
            take("w", 0, d - half)
            start_dn(0)
        ns_large()

        @pl.when(d < half)
        def _():
            end_up(1)
            give("u", 1, n + d, 1)

        @pl.when(d >= half)
        def _():
            end_dn(0)
            give("w", 0, d - half, 1)

    has_dn = (d == 0) | (d == 2)
    has_kv = (d >= 4) & (d < 7)
    dn_j = half + d // 2
    sq_j = 2 * jnp.where(d < half, d // 2, d - 2)
    kv_j = sq_count + d - half

    def round_c():
        @pl.when(has_dn)
        def _():
            take("w", 1, dn_j)
            start_dn(1)
            ns_large()
            end_dn(1)
            give("w", 1, dn_j, 2)

        size = xs.shape[1]

        @pl.when(jnp.logical_not(has_dn))
        def _():
            for s in range(2):
                take("s", s, sq_j + s)
                norm = frob(u_own["s"].at[s])
                xs[s] = (u_own["s"][s].astype(F32) / norm).astype(BF16).reshape(size, size)
            ns_small((0, 1), None)
            for s in range(2):
                u_own["s"][s] = xs[s].reshape(n, size // n, size)
                give("s", s, sq_j + s, 2 + s)

        @pl.when(has_kv)
        def _():
            take("s", 2, kv_j)
            u = jnp.transpose(u_own["s"][2].astype(F32).reshape(size, size))
            wide = size // PACK
            rows = jnp.sum(u * u, axis=1, keepdims=True)
            norm = jnp.concatenate(
                [jnp.broadcast_to(jnp.sum(rows[wide * k:wide * (k + 1)], axis=0, keepdims=True), (wide, 1))
                 for k in range(PACK)], axis=0)
            xs[2] = (u / (jnp.sqrt(norm) + EPS)).astype(BF16)
            mask = (lax.broadcasted_iota(jnp.int32, (size, size), 0) // wide
                    == lax.broadcasted_iota(jnp.int32, (size, size), 1) // wide)
            ns_small((2,), mask)
            u_own["s"][2] = jnp.transpose(xs[2].astype(F32)).astype(BF16).reshape(n, size // n, size)
            give("s", 2, kv_j, 4)

    def stage_d(q):
        f, j0, jm, j1 = GROUPS[q]
        for key in ("w" + f, "wk" if j1 > sq_count else None):
            if key in mw_loads:
                mw_loads.pop(key).wait()
        for j in range(j0, j1):
            dev, slot = OWNER[f][j]
            pl.when(d != dev)(lambda j=j: arrived(x_recv[f].at[j], sem_xr.at[FIRST[f] + j]))
        e1 = min(j1, sq_count) if f == "s" else j1

        def update(j, carry):
            w = wei[f][j]
            w = w - LR * (scale[f] * x_recv[f][j].astype(F32) + WD * w)
            wei[f][j] = w
            full[f][j, d] = w.astype(BF16)
            return carry
        lax.fori_loop(j0, e1, update, 0)
        if j1 > sq_count:
            wide = w_kv.shape[2]
            for i in range(j1 - sq_count):
                w = jnp.concatenate([wv_k[PACK * i + k] for k in range(PACK)], axis=-1)
                w = w - LR * (scale[f] * x_recv[f][sq_count + i].astype(F32) + WD * w)
                full[f][sq_count + i, d] = w.astype(BF16)
                for k in range(PACK):
                    wv_k[PACK * i + k] = w[:, wide * k:wide * (k + 1)]
        mine = full[f].at[pl.ds(j0, j1 - j0), d]
        send(mine, mine, sem_gs.at[q, 0], sem_gr.at[q, 0], right)
        send(mine, mine, sem_gs.at[q, 1], sem_gr.at[q, 1], left)
        send(mine, mine, sem_gs.at[q, 2], sem_gr.at[q, 2], peer)
        r = pl.ds(j0, e1 - j0)
        store(wei[f].at[r], out_w[f].at[r], sem_out.at[len(PIECES) + q, 0])
        if j1 > sq_count:
            store(wv_k, ow_kv, sem_out.at[len(PIECES) + q, 1])

    def stage_e(q):
        f, j0, jm, j1 = GROUPS[q]
        a, b, r = pl.ds(j0, jm - j0), pl.ds(jm, j1 - jm), pl.ds(j0, j1 - j0)
        arrived(full[f].at[r, left], sem_gr.at[q, 0])
        send(full[f].at[a, left], full[f].at[a, left], sem_gs.at[q, 3], sem_gr.at[q, 3], right)
        send(full[f].at[r, left], full[f].at[r, left], sem_gs.at[q, 5], sem_gr.at[q, 5], peer)
        arrived(full[f].at[r, right], sem_gr.at[q, 1])
        send(full[f].at[b, right], full[f].at[b, right], sem_gs.at[q, 4], sem_gr.at[q, 4], left)
        send(full[f].at[r, right], full[f].at[r, right], sem_gs.at[q, 6], sem_gr.at[q, 6], peer)

    def stage_h(q):
        f, j0, jm, j1 = GROUPS[q]
        far = 2 * xo + c
        for half_index, (lo, hi) in enumerate(((j0, jm), (jm, j1))):
            block = full[f].at[pl.ds(lo, hi - lo), far]
            arrived(block, sem_gr.at[q, 3 + half_index])
            send(block, block, sem_gs.at[q, 7 + half_index], sem_gr.at[q, 7 + half_index], peer)

    def stage_z(q):
        f, j0, jm, j1 = GROUPS[q]
        a, b, r = pl.ds(j0, jm - j0), pl.ds(jm, j1 - jm), pl.ds(j0, j1 - j0)
        oc = 1 - c
        arrived(full[f].at[r, peer], sem_gr.at[q, 2])
        arrived(full[f].at[r, 2 * xl + oc], sem_gr.at[q, 5])
        arrived(full[f].at[r, 2 * xr + oc], sem_gr.at[q, 6])
        arrived(full[f].at[a, 2 * xo + oc], sem_gr.at[q, 7])
        arrived(full[f].at[b, 2 * xo + oc], sem_gr.at[q, 8])
        e1 = min(j1, sq_count) if f == "s" else j1
        e = pl.ds(j0, e1 - j0)
        store(full[f].at[e], out_b[f].at[e], sem_outb.at[q, 0])
        if j1 > sq_count:
            size = fk.shape[1]
            for i in range(j1 - sq_count):
                fk[i] = jnp.transpose(full[f][sq_count + i].astype(F32).reshape(size, size)).astype(BF16)
            store(fk, ob_kv, sem_outb.at[q, 1])

    count = len(PIECES)
    after = {
        5: (round_a,),
        6: (lambda: stage_d(0),),
        7: (lambda: stage_d(1),),
        8: (lambda: stage_e(0),),
        9: (lambda: stage_e(1), round_b, lambda: stage_h(0)),
    }
    for i in range(-2, count):
        if i + 2 < count:
            stage_a(i + 2)
        if 0 <= i + 1 < count:
            stage_b(i + 1)
        if i >= 0:
            stage_c(i)
        for act in after.get(i, ()):
            act()
    stage_d(2)
    stage_d(3)
    stage_h(1)
    stage_z(0)
    round_c()
    stage_e(2)
    stage_e(3)
    for q in (4, 5, 6):
        stage_d(q)
    stage_z(1)
    for q in (2, 3):
        stage_h(q)
    for q in (4, 5, 6):
        stage_e(q)
    for q in (4, 5, 6):
        stage_h(q)
    for q in range(2, len(GROUPS)):
        stage_z(q)

    for copy, cond in sent:
        if cond is None:
            copy.wait_send()
        else:
            pl.when(cond)(copy.wait_send)
    given("u", 0, d, 0)
    pl.when(d < half)(lambda: given("u", 1, n + d, 1))
    pl.when(d >= half)(lambda: given("w", 0, d - half, 1))
    pl.when(has_dn)(lambda: given("w", 1, dn_j, 2))

    @pl.when(jnp.logical_not(has_dn))
    def _():
        given("s", 0, sq_j, 2)
        given("s", 1, sq_j + 1, 3)
    pl.when(has_kv)(lambda: given("s", 2, kv_j, 4))
    for copy in local:
        copy.wait()


def solution(mesh):
    n = mesh.shape["data"]
    nx = n // 2
    grad_spec = P(("model", "data"))
    slab_spec = P("model", "data")
    full_spec = P("model")

    def local_step(g_sq, m_sq, w_sq, g_kv, m_kv, w_kv, g_up, m_up, w_up, g_dn, m_dn, w_dn):
        def split(g, rows):
            return g[0].reshape(g.shape[1], nx, 2, rows, g.shape[3])

        sq, up, dn, kv = m_sq.shape, m_up.shape, m_dn.shape, m_kv.shape
        size = sq[2]
        packs = kv[0] // PACK
        small = sq[0] + packs
        grads = (
            split(g_sq, sq[1]),
            jnp.swapaxes(g_kv[0], 1, 2).reshape(packs, size, size),
            split(g_up, up[1]),
            split(g_dn, dn[1]),
        )
        fam = ((small,) + sq[1:], up, dn)

        def per(lead, dtype):
            return [pltpu.VMEM((shape[0],) + lead + shape[1:], dtype) for shape in fam]

        def own(slots):
            return [pltpu.VMEM((slot, n) + shape[1:], BF16) for slot, shape in zip(slots, fam)]

        dma = pltpu.SemaphoreType.DMA
        pieces, groups = len(PIECES), len(GROUPS)
        matrices = sum(shape[0] for shape in fam)
        scratch = (
            per((nx,), F32) + per((nx,), F32) + [pltpu.VMEM((packs, size, size), F32)] * 2
            + per((), F32) + per((), F32) + per((), F32)
            + [pltpu.VMEM(s, F32) for s in (fam[0], kv, up, dn)]
            + [pltpu.VMEM(s, F32) for s in (sq, kv, up, dn)]
            + per((), BF16) + own((3, 2, 2)) + per((), BF16) + per((n,), BF16)
            + [pltpu.VMEM((packs, size, size), BF16), pltpu.VMEM((n,) + up[1:], BF16), pltpu.VMEM((3, size, size), BF16)]
            + [dma((pieces,)), dma((8,)), dma((pieces,)), dma((pieces,)), dma((3,)), dma((pieces, 6)), dma((pieces, 6)),
               dma((matrices,)), dma((4, 3)), dma((5, n - 1)), dma((matrices,)), dma((groups, 9)), dma((groups, 9)),
               dma((pieces + groups, 2)), dma((groups, 2))]
        )

        def whole(shape):
            return (shape[0], n) + shape[1:]

        sds = jax.ShapeDtypeStruct
        out_shape = (
            sds(sq, F32), sds(sq, F32), sds(whole(sq), BF16),
            sds(kv, F32), sds(kv, F32), sds((packs, size, size), BF16),
            sds(up, F32), sds(up, F32), sds(whole(up), BF16),
            sds(dn, F32), sds(dn, F32), sds(whole(dn), BF16),
        )
        anywhere = pl.BlockSpec(memory_space=pl.ANY)

        def body(*refs):
            muon_kernel(n, nx, sq[0], *refs)

        res = pl.pallas_call(
            body,
            out_shape=out_shape,
            in_specs=[anywhere] * 12,
            out_specs=[anywhere] * 12,
            scratch_shapes=scratch,
            compiler_params=pltpu.CompilerParams(
                collective_id=0, has_side_effects=True, vmem_limit_bytes=62 * 1024 * 1024),
            name="muon",
        )(*grads, m_sq, m_kv, m_up, m_dn, w_sq, w_kv, w_up, w_dn)
        res = list(res)
        res[2] = res[2].reshape(sq[0], size, size)
        res[5] = jnp.swapaxes(res[5].reshape(kv[0], kv[2], size), 1, 2)
        res[8] = res[8].reshape(up[0], n * up[1], up[2])
        res[11] = res[11].reshape(dn[0], n * dn[1], dn[2])
        return tuple(res)

    in_specs = (grad_spec, slab_spec, slab_spec) * 4
    out_specs = (slab_spec, slab_spec, full_spec) * 4
    return jax.shard_map(local_step, mesh=mesh, in_specs=in_specs, out_specs=out_specs, check_vma=False)
```

time: 325 us -> 205 us (0.63)
  Pallas kernels: 0 us -> 186 us
  waiting for transfers between devices: 178 us -> 0 us
  blocking collectives: 55.5 us -> 0 us
  starting transfers between devices: 26 us -> 0 us
  matrix products: 15.5 us -> 0 us
  other arithmetic: 15.4 us -> 0 us
  between operations: 15.3 us -> 0.68 us
    pallas_call x0 -> x1, Pallas kernels: none -> 186 us  [local_step(): pl.pallas_call(body, out_shape=out_shape, in_specs=[anywhere] * 12, out_s...]
    reduce_scatter x4 -> x0, waiting for transfers between devices: 108 us -> none  [family_local(): lax.psum_scatter(grad_part[0], 'data', scatter_dimension=1, tiled=True)]
    all_to_all x3 -> x0, blocking collectives: 41.3 us -> none  [the longest x2 32.4 us: family_local(): lax.all_to_all(ortho.reshape(rounds, group_size, local_rows, columns), 'd...]
    all_to_all x5 -> x0, waiting for transfers between devices: 35.4 us -> none  [the longest x3 35.4 us: family_local(): lax.all_to_all(filled.reshape(rounds, group_size, local_rows, columns), '...]
    all_gather x3 -> x0, waiting for transfers between devices: 32.2 us -> none  [family_local(): lax.all_gather(weight_new.astype(jnp.bfloat16), 'data', axis=1, tiled=True)]
    all_to_all x5 -> x0, starting transfers between devices: 25.6 us -> none  [the longest x3 16.9 us: family_local(): lax.all_to_all(filled.reshape(rounds, group_size, local_rows, columns), '...]
    dot_general x40 -> x0, matrix products: 15.5 us -> none  [the longest x20 9.48 us: orthogonalize(): jnp.einsum(apply_form, poly_mat, ortho, preferred_element_type=jnp.float32)]
    all_gather x1 -> x0, blocking collectives: 14.2 us -> none  [family_local(): lax.all_gather(weight_new.astype(jnp.bfloat16), 'data', axis=1, tiled=True)]
  transfers between devices with their start and end apart: 12 -> 0, of which waited for: 7 -> 0; matrix products, arithmetic and copies ran while one was open for 12% -> 0% of each run, Pallas kernels for 0% -> 0%
where the time goes in v1:
time: 205 us
  Pallas kernels  186 us (91%)
  local copies, waits for them, and re-layouts  17.7 us (9%)
    pallas_call x1, Pallas kernels, local_step(): pl.pallas_call(body, out_shape=out_shape, in_specs=[anywhere] * 12, out_s...  186 us
    unnamed x32, local copies, waits for them, and re-layouts  17.7 us

profile of v1, /device:TPU:81, one launch (start us, length us, event | category | flops | bytes accessed | tf_op | source)
XLA Modules:
  0.0 204.5 jit_solution(12019839484130274985)
XLA Ops:
  0.6 186.1 %muon.1 = (f32[12,32,256]{2,1,0:T(8,128)}, f32[12,32,256]{2,1,0:T(8,128)}, bf16[12,8,32,256]{3,2,1,0:T(8,128)(2,1)}, f32[12,32,64]{2,1,0:T(8,128)}, f32[12,32,64...) custom-call(f32[12,4,2,32,256]{4,3,2,1,0:T(8,128)} %bitcast.17, ...), custom_call_target="tpu_custom_call" | custom-call | tf_op jit(solution)/shard_map/muon/pallas_call | solution.py:544
  186.8 0.0 copy-start.4
  186.8 1.9 copy.36
  188.6 0.0 copy-start.9
  188.7 0.0 copy-start.8
  188.7 1.8 copy.37
  190.5 0.0 copy-done.4
  190.5 0.0 copy-start.7
  190.5 0.0 copy-start.3
  190.5 0.0 copy-start.2
  190.5 1.1 copy.38
  191.6 0.0 copy-done.9
  191.6 0.7 copy.39
  192.3 0.0 copy-done.8
  192.3 0.7 copy.40
  193.0 0.0 copy-done.7
  193.0 0.0 copy-start
  193.0 0.7 copy.41
  193.7 0.0 copy-done.3
  193.7 1.1 copy.42
  194.9 0.0 copy-done.2
  194.9 1.1 copy.43
  196.0 1.1 copy-done
  197.1 0.0 copy-start.6
  197.1 0.0 copy-start.1
  197.1 3.2 %copy.44 = bf16[12,256,1024]{2,1,0:T(8,128)(2,1)} copy(bf16[12,256,1024]{2,1,0:T(8,128)(2,1)S(1)} %bitcast.16) | data formatting | bytes 12582912
  200.3 0.0 copy-done.6
  200.3 0.0 copy-start.5
  200.3 0.9 copy.45
  201.2 0.8 copy-done.5
  202.0 0.9 copy.46
  202.8 0.0 copy-done.1
  202.8 1.7 copy.47
Async XLA Ops:
  186.8 3.7 %copy-start.4 = (bf16[12,8,32,256]{3,2,1,0:T(8,128)(2,1)S(1)}, bf16[12,8,32,256]{3,2,1,0:T(8,128)(2,1)}, u32[]{:S(2)}) copy-start(bf16[12,8,32,256]{3,2,1,0:T(8,128)(2,1)} %get-tuple-element.26) | copy-start | bytes 4718596
  188.6 3.0 %copy-start.9 = (f32[12,32,64]{2,1,0:T(8,128)S(1)}, f32[12,32,64]{2,1,0:T(8,128)}, u32[]{:S(2)}) copy-start(f32[12,32,64]{2,1,0:T(8,128)} %get-tuple-element.51) | copy-start | bytes 294916
  188.7 3.7 %copy-start.8 = (f32[12,32,64]{2,1,0:T(8,128)S(1)}, f32[12,32,64]{2,1,0:T(8,128)}, u32[]{:S(2)}) copy-start(f32[12,32,64]{2,1,0:T(8,128)} %get-tuple-element.52) | copy-start | bytes 294916
  190.5 2.5 %copy-start.7 = (bf16[3,256,256]{2,1,0:T(8,128)(2,1)S(1)}, bf16[3,256,256]{2,1,0:T(8,128)(2,1)}, u32[]{:S(2)}) copy-start(bf16[3,256,256]{2,1,0:T(8,128)(2,1)} %get-tuple-element.29) | copy-start | bytes 1179652
  190.5 3.3 %copy-start.3 = (f32[12,32,1024]{2,1,0:T(8,128)S(1)}, f32[12,32,1024]{2,1,0:T(8,128)}, u32[]{:S(2)}) copy-start(f32[12,32,1024]{2,1,0:T(8,128)} %get-tuple-element.54) | copy-start | bytes 4718596
  190.5 4.4 %copy-start.2 = (f32[12,32,1024]{2,1,0:T(8,128)S(1)}, f32[12,32,1024]{2,1,0:T(8,128)}, u32[]{:S(2)}) copy-start(f32[12,32,1024]{2,1,0:T(8,128)} %get-tuple-element.55) | copy-start | bytes 4718596
  193.0 4.1 %copy-start = (bf16[12,8,32,1024]{3,2,1,0:T(8,128)(2,1)S(1)}, bf16[12,8,32,1024]{3,2,1,0:T(8,128)(2,1)}, u32[]{:S(2)}) copy-start(bf16[12,8,32,1024]{3,2,1,0:T(8,128)(2,1)} %get-tuple-element.32) | copy-start | bytes 18874372
  197.1 3.2 %copy-start.6 = (f32[6,128,256]{2,1,0:T(8,128)S(1)}, f32[6,128,256]{2,1,0:T(8,128)}, u32[]{:S(2)}) copy-start(f32[6,128,256]{2,1,0:T(8,128)} %get-tuple-element.57) | copy-start | bytes 2359300
  197.1 5.8 %copy-start.1 = (bf16[6,8,128,256]{3,2,1,0:T(8,128)(2,1)S(1)}, bf16[6,8,128,256]{3,2,1,0:T(8,128)(2,1)}, u32[]{:S(2)}) copy-start(bf16[6,8,128,256]{3,2,1,0:T(8,128)(2,1)} %get-tuple-element.35) | copy-start | bytes 9437188
  200.3 1.7 copy-start.5

commit v2 on v1

--- a/solution.py
+++ b/solution.py
@@ -26,7 +26,7 @@
     ("w", 0, 1, 2), ("w", 2, 3, 4), ("w", 4, 5, 6), ("s", 0, 4, 8), ("s", 8, 12, 15),
 )
 GROUPS = (
-    ("u", 0, 2, 4), ("u", 4, 6, 8), ("u", 8, 10, 12), ("w", 0, 2, 4), ("w", 4, 5, 6), ("s", 0, 4, 8), ("s", 8, 12, 15),
+    ("u", 0, 0, 4), ("u", 4, 4, 8), ("u", 8, 8, 12), ("w", 0, 0, 4), ("w", 4, 4, 6), ("s", 0, 0, 8), ("s", 8, 8, 15),
 )
 OWNER = {
     "u": tuple((j, 0) for j in range(8)) + tuple((j, 1) for j in range(4)),
@@ -39,13 +39,12 @@
 
 def muon_kernel(n, nx, sq_count, *refs):
     (g_sq, g_kv, g_up, g_dn, m_sq, m_kv, m_up, m_dn, w_sq, w_kv, w_up, w_dn,
-     om_sq, ow_sq, ob_sq, om_kv, ow_kv, ob_kv, om_up, ow_up, ob_up, om_dn, ow_dn, ob_dn,
+     mv_s, wv_s, f_s, mv_k, wv_k, fk, mv_u, wv_u, f_u, mv_w, wv_w, f_w,
      p_s, p_u, p_w, q_s, q_u, q_w, pk, qk,
      t_s, t_u, t_w, l_s, l_u, l_w, r_s, r_u, r_w,
-     mv_s, mv_k, mv_u, mv_w, wv_s, wv_k, wv_u, wv_w,
-     us_s, us_u, us_w, uo_s, uo_u, uo_w, xr_s, xr_u, xr_w, f_s, f_u, f_w, fk, xt, xs,
+     us_s, us_u, us_w, uo_s, uo_u, uo_w, xr_s, xr_u, xr_w, xt, xs,
      sem_load, sem_mw, sem_peer_s, sem_peer_r, sem_kv, sem_st_s, sem_st_r, sem_us, sem_ur,
-     sem_xs, sem_xr, sem_gs, sem_gr, sem_out, sem_outb) = refs
+     sem_xs, sem_xr, sem_gs, sem_gr) = refs
     part = {"s": p_s, "u": p_u, "w": p_w}
     other = {"s": q_s, "u": q_u, "w": q_w}
     opp = {"s": t_s, "u": t_u, "w": t_w}
@@ -58,9 +57,6 @@
     u_own = {"s": uo_s, "u": uo_u, "w": uo_w}
     x_recv = {"s": xr_s, "u": xr_u, "w": xr_w}
     full = {"s": f_s, "u": f_u, "w": f_w}
-    out_m = {"s": om_sq, "u": om_up, "w": om_dn}
-    out_w = {"s": ow_sq, "u": ow_up, "w": ow_dn}
-    out_b = {"s": ob_sq, "u": ob_up, "w": ob_dn}
     scale = {
         "s": 0.2 * math.sqrt(n * m_sq.shape[1]),
         "u": 0.2 * math.sqrt(m_up.shape[2]),
@@ -91,13 +87,6 @@
         else:
             pl.when(cond)(copy.start)
         sent.append((copy, cond))
-
-    local = []
-
-    def store(src, dst, sem):
-        copy = pltpu.make_async_copy(src, dst, sem)
-        copy.start()
-        local.append(copy)
 
     loads = []
     for p, (f, j0, jm, j1) in enumerate(PIECES):
@@ -194,14 +183,10 @@
         for j in range(j0, j1):
             dev, slot = OWNER[f][j]
             send(u_send[f].at[j], u_own[f].at[slot, d], sem_us.at[FIRST[f] + j], sem_ur.at[FIRST[f] // 6, slot], dev, d != dev)
-        e1 = min(j1, sq_count) if f == "s" else j1
-        r = pl.ds(j0, e1 - j0)
-        store(mom[f].at[r], out_m[f].at[r], sem_out.at[p, 0])
         if j1 > sq_count:
             for i in range(j1 - sq_count):
                 for k in range(PACK):
                     mv_k[PACK * i + k] = mv_s[sq_count + i, :, wide * k:wide * (k + 1)]
-            store(mv_k, om_kv, sem_out.at[p, 1])
 
     def take(f, slot, j):
         rows = u_own[f].at[slot, pl.ds(0, n - 1)]
@@ -386,25 +371,25 @@
         send(mine, mine, sem_gs.at[q, 0], sem_gr.at[q, 0], right)
         send(mine, mine, sem_gs.at[q, 1], sem_gr.at[q, 1], left)
         send(mine, mine, sem_gs.at[q, 2], sem_gr.at[q, 2], peer)
-        r = pl.ds(j0, e1 - j0)
-        store(wei[f].at[r], out_w[f].at[r], sem_out.at[len(PIECES) + q, 0])
-        if j1 > sq_count:
-            store(wv_k, ow_kv, sem_out.at[len(PIECES) + q, 1])
 
     def stage_e(q):
         f, j0, jm, j1 = GROUPS[q]
         a, b, r = pl.ds(j0, jm - j0), pl.ds(jm, j1 - jm), pl.ds(j0, j1 - j0)
         arrived(full[f].at[r, left], sem_gr.at[q, 0])
-        send(full[f].at[a, left], full[f].at[a, left], sem_gs.at[q, 3], sem_gr.at[q, 3], right)
+        if jm > j0:
+            send(full[f].at[a, left], full[f].at[a, left], sem_gs.at[q, 3], sem_gr.at[q, 3], right)
         send(full[f].at[r, left], full[f].at[r, left], sem_gs.at[q, 5], sem_gr.at[q, 5], peer)
         arrived(full[f].at[r, right], sem_gr.at[q, 1])
-        send(full[f].at[b, right], full[f].at[b, right], sem_gs.at[q, 4], sem_gr.at[q, 4], left)
+        if j1 > jm:
+            send(full[f].at[b, right], full[f].at[b, right], sem_gs.at[q, 4], sem_gr.at[q, 4], left)
         send(full[f].at[r, right], full[f].at[r, right], sem_gs.at[q, 6], sem_gr.at[q, 6], peer)
 
     def stage_h(q):
         f, j0, jm, j1 = GROUPS[q]
         far = 2 * xo + c
         for half_index, (lo, hi) in enumerate(((j0, jm), (jm, j1))):
+            if hi == lo:
+                continue
             block = full[f].at[pl.ds(lo, hi - lo), far]
             arrived(block, sem_gr.at[q, 3 + half_index])
             send(block, block, sem_gs.at[q, 7 + half_index], sem_gr.at[q, 7 + half_index], peer)
@@ -416,16 +401,14 @@
         arrived(full[f].at[r, peer], sem_gr.at[q, 2])
         arrived(full[f].at[r, 2 * xl + oc], sem_gr.at[q, 5])
         arrived(full[f].at[r, 2 * xr + oc], sem_gr.at[q, 6])
-        arrived(full[f].at[a, 2 * xo + oc], sem_gr.at[q, 7])
-        arrived(full[f].at[b, 2 * xo + oc], sem_gr.at[q, 8])
-        e1 = min(j1, sq_count) if f == "s" else j1
-        e = pl.ds(j0, e1 - j0)
-        store(full[f].at[e], out_b[f].at[e], sem_outb.at[q, 0])
+        if jm > j0:
+            arrived(full[f].at[a, 2 * xo + oc], sem_gr.at[q, 7])
+        if j1 > jm:
+            arrived(full[f].at[b, 2 * xo + oc], sem_gr.at[q, 8])
         if j1 > sq_count:
             size = fk.shape[1]
             for i in range(j1 - sq_count):
                 fk[i] = jnp.transpose(full[f][sq_count + i].astype(F32).reshape(size, size)).astype(BF16)
-            store(fk, ob_kv, sem_outb.at[q, 1])
 
     count = len(PIECES)
     after = {
@@ -478,7 +461,19 @@
         given("s", 0, sq_j, 2)
         given("s", 1, sq_j + 1, 3)
     pl.when(has_kv)(lambda: given("s", 2, kv_j, 4))
-    for copy in local:
+
+def write_kernel(*refs):
+    sources, results, sem = refs[:12], refs[12:24], refs[24]
+    copies = []
+    for i, (src, dst) in enumerate(zip(sources, results)):
+        count = dst.shape[0]
+        step = count if len(dst.shape) == 3 else max(1, count // 3)
+        for k, j in enumerate(range(0, count, step)):
+            r = pl.ds(j, step)
+            copies.append(pltpu.make_async_copy(src.at[r], dst.at[r], sem.at[i, k]))
+    for copy in copies:
+        copy.start()
+    for copy in copies:
         copy.wait()
 
 
@@ -517,13 +512,10 @@
         scratch = (
             per((nx,), F32) + per((nx,), F32) + [pltpu.VMEM((packs, size, size), F32)] * 2
             + per((), F32) + per((), F32) + per((), F32)
-            + [pltpu.VMEM(s, F32) for s in (fam[0], kv, up, dn)]
-            + [pltpu.VMEM(s, F32) for s in (sq, kv, up, dn)]
-            + per((), BF16) + own((3, 2, 2)) + per((), BF16) + per((n,), BF16)
-            + [pltpu.VMEM((packs, size, size), BF16), pltpu.VMEM((n,) + up[1:], BF16), pltpu.VMEM((3, size, size), BF16)]
+            + per((), BF16) + own((3, 2, 2)) + per((), BF16)
+            + [pltpu.VMEM((n,) + up[1:], BF16), pltpu.VMEM((3, size, size), BF16)]
             + [dma((pieces,)), dma((8,)), dma((pieces,)), dma((pieces,)), dma((3,)), dma((pieces, 6)), dma((pieces, 6)),
-               dma((matrices,)), dma((4, 3)), dma((5, n - 1)), dma((matrices,)), dma((groups, 9)), dma((groups, 9)),
-               dma((pieces + groups, 2)), dma((groups, 2))]
+               dma((matrices,)), dma((4, 3)), dma((5, n - 1)), dma((matrices,)), dma((groups, 9)), dma((groups, 9))]
         )
 
         def whole(shape):
@@ -536,21 +528,37 @@
             sds(up, F32), sds(up, F32), sds(whole(up), BF16),
             sds(dn, F32), sds(dn, F32), sds(whole(dn), BF16),
         )
+        held = (
+            (fam[0], F32), (sq, F32), (whole(fam[0]), BF16),
+            (kv, F32), (kv, F32), ((packs, size, size), BF16),
+            (up, F32), (up, F32), (whole(up), BF16),
+            (dn, F32), (dn, F32), (whole(dn), BF16),
+        )
         anywhere = pl.BlockSpec(memory_space=pl.ANY)
+        inside = pl.BlockSpec(memory_space=pltpu.VMEM)
 
         def body(*refs):
             muon_kernel(n, nx, sq[0], *refs)
 
         res = pl.pallas_call(
             body,
-            out_shape=out_shape,
+            out_shape=[pltpu.VMEM(shape, dtype) for shape, dtype in held],
             in_specs=[anywhere] * 12,
-            out_specs=[anywhere] * 12,
+            out_specs=[inside] * 12,
             scratch_shapes=scratch,
             compiler_params=pltpu.CompilerParams(
-                collective_id=0, has_side_effects=True, vmem_limit_bytes=62 * 1024 * 1024),
+                collective_id=0, has_side_effects=True, vmem_limit_bytes=44 * 1024 * 1024),
             name="muon",
         )(*grads, m_sq, m_kv, m_up, m_dn, w_sq, w_kv, w_up, w_dn)
+        res = pl.pallas_call(
+            write_kernel,
+            out_shape=out_shape,
+            in_specs=[inside] * 12,
+            out_specs=[anywhere] * 12,
+            scratch_shapes=[dma((12, 3))],
+            compiler_params=pltpu.CompilerParams(vmem_limit_bytes=2 * 1024 * 1024),
+            name="write",
+        )(*(pltpu.with_memory_space_constraint(r, pltpu.VMEM) for r in res))
         res = list(res)
         res[2] = res[2].reshape(sq[0], size, size)
         res[5] = jnp.swapaxes(res[5].reshape(kv[0], kv[2], size), 1, 2)

time: 205 us -> 204 us (level)
  Pallas kernels: 186 us -> 204 us
  local copies, waits for them, and re-layouts: 17.7 us -> 0 us
    unnamed x32 -> x0, local copies, waits for them, and re-layouts: 17.7 us -> none
    pallas_call x1 -> x2, Pallas kernels: 186 us -> 204 us  [the longest x1 197 us: local_step(): pl.pallas_call(body, out_shape=[pltpu.VMEM(shape, dtype) for shape, dtype...]
where the time goes in v2:
time: 204 us
  Pallas kernels  204 us (100%)
    pallas_call x1, Pallas kernels, local_step(): pl.pallas_call(body, out_shape=[pltpu.VMEM(shape, dtype) for shape, dtype...  197 us
    pallas_call x1, Pallas kernels, local_step(): pl.pallas_call(write_kernel, out_shape=out_shape, in_specs=[inside] * 12,...  6.32 us

profile of v2, /device:TPU:81, one launch (start us, length us, event | category | flops | bytes accessed | tf_op | source)
XLA Modules:
  0.0 204.3 jit_solution(13654298932719686224)
XLA Ops:
  0.6 197.3 %muon.1 = (f32[15,32,256]{2,1,0:T(8,128)S(1)}, f32[12,32,256]{2,1,0:T(8,128)S(1)}, bf16[15,8,32,256]{3,2,1,0:T(8,128)(2,1)S(1)}, f32[12,32,64]{2,1,0:T(8,128)S(1...) custom-call(f32[12,4,2,32,256]{4,3,2,1,0:T(8,128)} %bitcast.16, ...), custom_call_target="tpu_custom_call" | custom-call | tf_op jit(solution)/shard_map/muon/pallas_call | solution.py:543
  198.0 6.3 %write.1 = (f32[12,32,256]{2,1,0:T(8,128)}, f32[12,32,256]{2,1,0:T(8,128)}, bf16[12,8,32,256]{3,2,1,0:T(8,128)(2,1)}, f32[12,32,64]{2,1,0:T(8,128)}, f32[12,32,6...) custom-call(f32[15,32,256]{2,1,0:T(8,128)S(1)} %get-tuple-element.36, ...), custom_call_target="tpu_custom_call" | custom-call | tf_op jit(solution)/shard_map/write/pallas_call | solution.py:553

commit v3 on v2

--- a/solution.py
+++ b/solution.py
@@ -26,7 +26,7 @@
     ("w", 0, 1, 2), ("w", 2, 3, 4), ("w", 4, 5, 6), ("s", 0, 4, 8), ("s", 8, 12, 15),
 )
 GROUPS = (
-    ("u", 0, 0, 4), ("u", 4, 4, 8), ("u", 8, 8, 12), ("w", 0, 0, 4), ("w", 4, 4, 6), ("s", 0, 0, 8), ("s", 8, 8, 15),
+    ("u", 0, 4, 4), ("u", 4, 8, 8), ("u", 8, 12, 12), ("w", 0, 4, 4), ("w", 4, 6, 6), ("s", 0, 8, 8), ("s", 8, 15, 15),
 )
 OWNER = {
     "u": tuple((j, 0) for j in range(8)) + tuple((j, 1) for j in range(4)),
@@ -34,7 +34,6 @@
     "s": tuple((dev, slot) for dev in (1, 3, 4, 5, 6, 7) for slot in (0, 1)) + ((4, 2), (5, 2), (6, 2)),
 }
 FIRST = {"u": 0, "w": 12, "s": 18}
-PEER_SEMS = 6
 
 
 def muon_kernel(n, nx, sq_count, *refs):
@@ -409,6 +408,17 @@
             size = fk.shape[1]
             for i in range(j1 - sq_count):
                 fk[i] = jnp.transpose(full[f][sq_count + i].astype(F32).reshape(size, size)).astype(BF16)
+
+    def scoped(name, fn):
+        def run(*args):
+            with jax.named_scope("_".join([name] + [str(a) for a in args])):
+                fn(*args)
+        return run
+
+    stage_a, stage_b, stage_c = scoped("reduce_a", stage_a), scoped("reduce_b", stage_b), scoped("update_c", stage_c)
+    stage_d, stage_e = scoped("weights_d", stage_d), scoped("forward_e", stage_e)
+    stage_h, stage_z = scoped("across_h", stage_h), scoped("finish_z", stage_z)
+    round_a, round_b, round_c = scoped("round_a", round_a), scoped("round_b", round_b), scoped("round_c", round_c)
 
     count = len(PIECES)
     after = {

time: 204 us -> 205 us (level)
  no operation moved by 1% of the time
where the time goes in v3:
time: 205 us
  Pallas kernels  205 us (100%)
    pallas_call x1, Pallas kernels, local_step(): pl.pallas_call(body, out_shape=[pltpu.VMEM(shape, dtype) for shape, dtype...  198 us
    pallas_call x1, Pallas kernels, local_step(): pl.pallas_call(write_kernel, out_shape=out_shape, in_specs=[inside] * 12,...  6.32 us

profile of v3, /device:TPU:81, one launch (start us, length us, event | category | flops | bytes accessed | tf_op | source)
XLA Modules:
  0.0 205.2 jit_solution(7084973146521654340)
XLA Ops:
  0.6 198.2 %muon.1 = (f32[15,32,256]{2,1,0:T(8,128)S(1)}, f32[12,32,256]{2,1,0:T(8,128)S(1)}, bf16[15,8,32,256]{3,2,1,0:T(8,128)(2,1)S(1)}, f32[12,32,64]{2,1,0:T(8,128)S(1...) custom-call(f32[12,4,2,32,256]{4,3,2,1,0:T(8,128)} %bitcast.16, ...), custom_call_target="tpu_custom_call" | custom-call | tf_op jit(solution)/shard_map/muon/pallas_call | solution.py:553
  198.9 6.3 %write.1 = (f32[12,32,256]{2,1,0:T(8,128)}, f32[12,32,256]{2,1,0:T(8,128)}, bf16[12,8,32,256]{3,2,1,0:T(8,128)(2,1)}, f32[12,32,64]{2,1,0:T(8,128)}, f32[12,32,6...) custom-call(f32[15,32,256]{2,1,0:T(8,128)S(1)} %get-tuple-element.36, ...), custom_call_target="tpu_custom_call" | custom-call | tf_op jit(solution)/shard_map/write/pallas_call | solution.py:563
